TPU v7x, 32 devices: a whole 2x2x4 slice. The times are simulated.
32 devices in a mesh: grp: 4 (over z), freq: 8 (over y, x, core).
Axes of the slice: x: 2, y: 2, z: 4, core: 2. Of those that a mesh axis runs over, the one named last changes fastest.
Arguments:
- sources: bfloat16 [1024, 32768], P('freq', 'grp'), may hold values from -6 to 6
- panel_pos: float32 [3, 32768], P(None, 'grp'), may hold values from -1 to 1
- panel_blade: int32 [32768], P('grp'), may hold values from 0 to 3
- observer_table: float32 [3, 2048], replicated, may hold values from -8 to 8, as said below
- observer_index: int32 [32], replicated, may hold values from 0 to 2047
Outputs:
- spectra: float32 [512, 4, 2, 32], P('freq', 'grp')
Inputs may be any that keep to these rules, and one draw needn't show every extreme that they name: `observer_table`: each observer lies 3 to 8 units from the anchor (0, 0, 0).
All inputs are finite; a program needn't handle non-finite values.
Results may differ from a plain program's by a relative error of at most 0.0047.
Values may be sent and summed in bfloat16 or wider, within the bound.
A program may use at most 64 MiB of HBM per device.

v0:
```python
import math
import jax
import jax.numpy as jnp
from jax import lax
from jax.sharding import PartitionSpec as P

NT = 1024
NF = 512
NCOMP = 4
wave_step = 0.04


def transform_table():
    row_index = jnp.arange(2 * NF, dtype=jnp.int32)
    samples = jnp.arange(NT, dtype=jnp.int32)
    frequency = row_index // 2
    parity = row_index % 2
    turn_count = frequency[:, None] * samples[None, :] % NT
    angle_table = 2.0 * math.pi / NT * turn_count.astype(jnp.float32)
    values = jnp.where(parity[:, None] == 0, jnp.cos(angle_table), -jnp.sin(angle_table))
    return (values / math.sqrt(NT)).astype(jnp.bfloat16)


def distances(positions, observers):
    offset_x = observers[0][:, None] - positions[0][None, :]
    offset_y = observers[1][:, None] - positions[1][None, :]
    offset_z = observers[2][:, None] - positions[2][None, :]
    return jnp.sqrt(offset_x * offset_x + offset_y * offset_y + offset_z * offset_z)


def blade_masks(blades):
    return (blades[None, :] == jnp.arange(NCOMP, dtype=jnp.int32)[:, None]).astype(jnp.bfloat16)


def frequency_term(frequency, spectrum_pair, blade_mask, distance, amplitude):
    wavenumber = wave_step * frequency.astype(jnp.float32)
    phase_angle = wavenumber * distance
    green_matrix = jnp.concatenate(
        [jnp.cos(phase_angle) * amplitude, -jnp.sin(phase_angle) * amplitude], axis=0
    ).astype(jnp.bfloat16)
    weighted = jnp.concatenate(
        [spectrum_pair[0][None, :] * blade_mask, spectrum_pair[1][None, :] * blade_mask], axis=0
    )
    product = lax.dot_general(
        weighted, green_matrix, (((1,), (1,)), ((), ())), preferred_element_type=jnp.float32
    )
    blade_count = blade_mask.shape[0]
    observer_count = distance.shape[0]
    real_part = product[:blade_count, :observer_count] - product[blade_count:, observer_count:]
    imag_part = product[:blade_count, observer_count:] + product[blade_count:, :observer_count]
    return jnp.stack([real_part, imag_part], axis=1)


def body(sources, panel_pos, panel_blade, observer_table, observer_index):
    freq_share = NF // lax.axis_size("freq")
    position = lax.axis_index("freq")
    observers = observer_table[:, observer_index]
    dft_table = transform_table()
    device_count = lax.axis_size("freq")
    shaped = sources.reshape(sources.shape[0], device_count, sources.shape[1] // device_count)
    piece = lax.all_to_all(shaped, "freq", split_axis=1, concat_axis=0, tiled=True)
    item_count = piece.shape[2]
    flat = piece.reshape(piece.shape[0], item_count)
    local_spec = jnp.dot(dft_table, flat, preferred_element_type=jnp.float32).astype(jnp.bfloat16)
    gathered = lax.all_to_all(
        local_spec.reshape(2 * NF, 1, item_count), "freq", split_axis=0, concat_axis=1, tiled=True
    )
    received = gathered.reshape(gathered.shape[0], gathered.shape[1] * gathered.shape[2])
    spectra_pairs = received.reshape(freq_share, 2, received.shape[1])
    distance = distances(panel_pos, observers)
    amplitude = 0.25 / (math.pi * distance)
    blade_mask = blade_masks(panel_blade)
    frequencies = position * freq_share + jnp.arange(freq_share, dtype=jnp.int32)

    def per_frequency(element):
        return frequency_term(element[0], element[1], blade_mask, distance, amplitude)

    partial_value = lax.map(per_frequency, (frequencies, spectra_pairs))
    summed = lax.psum(partial_value, "grp")
    blade_share = NCOMP // lax.axis_size("grp")
    return lax.dynamic_slice_in_dim(summed, lax.axis_index("grp") * blade_share, blade_share, 1)


def solution(mesh):
    in_specs = (P("freq", "grp"), P(None, "grp"), P("grp"), P(), P())
    out_specs = P("freq", "grp", None, None)
    return jax.shard_map(body, mesh=mesh, in_specs=in_specs, out_specs=out_specs, check_vma=False)
```

profile of v0, /device:TPU:0, one launch (start us, length us, event | category | flops | bytes accessed | tf_op | source)
XLA Modules:
  0.0 632.9 jit_solution(9008926720111402404)
XLA Ops:
  10.6 5.2 all-to-all-start
  17.1 25.4 %all-to-all-done = bf16[128,8,1024]{0,2,1:T(8,128)(2,1)S(1)} async-done(((bf16[128,8,1024]{0,2,1:T(8,128)(2,1)}), bf16[128,8,1024]{0,2,1:T(8,128)(2,1)S(1)}, u32[]{:S(2)}, u32[]{:S(2)}) %all-to-all-start) | async-done | bytes 2097184 | tf_op jit(solution)/shard_map/all_to_all | solution.py:61
  45.1 22.1 %convert_bitcast_fusion = bf16[1024,1,1024]{2,0,1:T(8,128)(2,1)} fusion(bf16[1024,1024]{1,0:T(8,128)(2,1)} %bitcast.37, s32[1024]{0:T(1024)S(1)} %add_select_fusion.1, pred[1024]{0:T(1024)(128)(4,1)S(1)} %fusion.32), kind=kOutput, calls=%fused_computation.37 | convolution fusion | flops 2167406592 | bytes 4199424 | tf_op jit(solution)/shard_map/dot_general | solution.py:64
  79.4 26.2 %all-to-all-done.1 = bf16[8,2,65536]{2,1,0:T(2,128)(2,1)S(1)} async-done(((bf16[8,2,65536]{2,1,0:T(2,128)(2,1)}), bf16[8,2,65536]{2,1,0:T(2,128)(2,1)S(1)}, u32[]{:S(2)}, u32[]{:S(2)}) %all-to-all-start.1) | async-done | bytes 2097184 | tf_op jit(solution)/shard_map/all_to_all | solution.py:65
  117.0 472.7 %while.12 = (s32[]{:T(128)}, f32[64,4,2,32]{3,1,2,0:T(4,128)S(1)}, bf16[64,2,8192]{2,1,0:T(2,128)(2,1)}, s32[64]{0:T(128)S(1)}, s32[8192]{0:T(1024)S(1)}, /*inde...) while((s32[]{:T(128)}, f32[64,4,2,32]{3,1,2,0:T(4,128)S(1)}, ...), condition=%wide.region_1.2_spmd.clone.clone, body=%wide.region_0.1_spmd.clone.clone.sunk | while | flops 15041029 | bytes 2602569 | solution.py:78
  118.2 4.6 multiply_convert_fusion.7
  147.7 4.6 multiply_convert_fusion.7
  155.1 4.6 multiply_convert_fusion.7
  184.7 4.6 multiply_convert_fusion.7
  192.0 4.6 multiply_convert_fusion.7
  214.2 4.6 multiply_convert_fusion.7
  221.6 4.6 multiply_convert_fusion.7
  251.1 4.6 multiply_convert_fusion.7
  258.5 4.6 multiply_convert_fusion.7
  288.1 4.6 multiply_convert_fusion.7
  295.4 4.6 multiply_convert_fusion.7
  325.0 4.6 multiply_convert_fusion.7
  332.4 4.6 multiply_convert_fusion.7
  354.5 4.6 multiply_convert_fusion.7
  361.9 4.6 multiply_convert_fusion.7
  391.5 4.6 multiply_convert_fusion.7
  398.9 4.6 multiply_convert_fusion.7
  428.4 4.6 multiply_convert_fusion.7
  435.8 4.6 multiply_convert_fusion.7
  465.3 4.6 multiply_convert_fusion.7
  472.7 4.6 multiply_convert_fusion.7
  494.9 4.6 multiply_convert_fusion.7
  502.3 4.6 multiply_convert_fusion.7
  531.8 4.6 multiply_convert_fusion.7
  539.2 4.6 multiply_convert_fusion.7
  568.7 4.6 multiply_convert_fusion.7
  590.5 34.2 %all-reduce.2.cloned.1.call-done = f32[64,4,2,32]{0,3,2,1:T(8,128)} async-done(((f32[64,4,2,32]{0,3,2,1:T(8,128)}), f32[64,4,2,32]{0,3,2,1:T(8,128)}) %all-reduce.2.cloned.1.call-update) | async-done | bytes 65552 | tf_op jit(solution)/shard_map/psum | solution.py:79
  (454 shorter events, 345.9 us)
Async XLA Ops:
  6.5 9.3 %copy-start.2 = (f32[3,2048]{1,0:T(4,128)S(1)}, f32[3,2048]{1,0:T(4,128)}, u32[]{:S(2)}) copy-start(f32[3,2048]{1,0:T(4,128)} %param.10) | copy-start | bytes 73732
  6.5 9.7 %copy-start.3 = (s32[32]{0:T(128)S(1)}, s32[32]{0:T(128)}, u32[]{:S(2)}) copy-start(s32[32]{0:T(128)} %param.11) | copy-start | bytes 388
  10.6 31.8 %all-to-all-start = ((bf16[128,8,1024]{0,2,1:T(8,128)(2,1)}), bf16[128,8,1024]{0,2,1:T(8,128)(2,1)S(1)}, u32[]{:S(2)}, u32[]{:S(2)}) async-start(bf16[128,8,1024]{0,2,1:T(8,128)(2,1)} %bitcast.36), calls=%async_computation | async-start | bytes 4194304 | tf_op jit(solution)/shard_map/all_to_all | solution.py:61
  71.6 7.7 %copy-start.1 = (f32[3,8192]{1,0:T(4,128)S(1)}, f32[3,8192]{1,0:T(4,128)}, u32[]{:S(2)}) copy-start(f32[3,8192]{1,0:T(4,128)} %param.8) | copy-start | bytes 294916
  75.4 30.2 %all-to-all-start.1 = ((bf16[8,2,65536]{2,1,0:T(2,128)(2,1)}), bf16[8,2,65536]{2,1,0:T(2,128)(2,1)S(1)}, u32[]{:S(2)}, u32[]{:S(2)}) async-start(bf16[8,2,65536]{2,1,0:T(2,128)(2,1)} %reshape.63), calls=%async_computation.1 | async-start | bytes 4194304 | tf_op jit(solution)/shard_map/all_to_all | solution.py:65
  79.1 545.6 %all-reduce.2.cloned.1.call-start = ((), (), s32[]{:S(2)}) async-start(), calls=%async_computation.2 | async-start | bytes 262144 | tf_op jit(solution)/shard_map/psum | solution.py:79
  113.0 4.0 copy-start
Sparse Core Ops, SparseCore 0:
  590.6 34.0 all-reduce.1
where the time goes:
time: 639 us; the launch traced here: 633 us
  other arithmetic  307 us (48%)
  local copies, waits for them, and re-layouts  130 us (20%)
  waiting for transfers between devices  85.8 us (13%)
  matrix products  46 us (7%)
  loops' own time  41.1 us (6%)
  between operations  13.5 us (2%)
  starting transfers between devices  9.02 us (1%)
    another operation x64, other arithmetic  294 us
    slice x64, local copies, waits for them, and re-layouts, frequency_term(): spectrum_pair[0][None, :] * blade_mask  65.3 us
    another operation x1, loops' own time, body(): partial_value = lax.map(per_frequency, (frequencies, spectra_pairs))  41.1 us
    dynamic_slice x64, local copies, waits for them, and re-layouts, body(): partial_value = lax.map(per_frequency, (frequencies, spectra_pairs))  38.9 us
    psum x1, waiting for transfers between devices, body(): summed = lax.psum(partial_value, 'grp')  34.2 us
    all_to_all x1, waiting for transfers between devices, body(): lax.all_to_all(local_spec.reshape(2 * NF, 1, item_count), 'freq', split_a...  26.2 us
    all_to_all x1, waiting for transfers between devices, body(): lax.all_to_all(shaped, 'freq', split_axis=1, concat_axis=0, tiled=True)  25.4 us
    dot_general x64, matrix products, frequency_term(): lax.dot_general(weighted, green_matrix, (((1,), (1,)), ((), ())), preferr...  23.9 us
  transfers between devices with their start and end apart: 3, of which 3 were waited for; matrix products, arithmetic and copies ran while one was open for 0% of the time, Pallas kernels for 0%

commit v1 on v0

--- a/solution.py
+++ b/solution.py
@@ -76,7 +76,7 @@
         return frequency_term(element[0], element[1], blade_mask, distance, amplitude)
 
     partial_value = lax.map(per_frequency, (frequencies, spectra_pairs))
-    summed = lax.psum(partial_value, "grp")
+    summed = jnp.sum(lax.all_gather(partial_value, "grp"), axis=0)
     blade_share = NCOMP // lax.axis_size("grp")
     return lax.dynamic_slice_in_dim(summed, lax.axis_index("grp") * blade_share, blade_share, 1)
 

time: 639 us -> 612 us (0.958)
  waiting for transfers between devices: 85.8 us -> 51.6 us
  blocking collectives: 0 us -> 21.5 us
  between operations: 13.5 us -> 0.15 us
    psum x1 -> x0, waiting for transfers between devices: 34.2 us -> none  [body(): summed = lax.psum(partial_value, 'grp')]
    all_gather x0 -> x1, blocking collectives: none -> 21.5 us  [body(): summed = jnp.sum(lax.all_gather(partial_value, 'grp'), axis=0)]
  transfers between devices with their start and end apart: 3 -> 2, of which waited for: 3 -> 2; matrix products, arithmetic and copies ran while one was open for 0% -> 0% of each run, Pallas kernels for 0% -> 0%
where the time goes in v1:
time: 612 us; the launch traced here: 606 us
  other arithmetic  308 us (50%)
  local copies, waits for them, and re-layouts  129 us (21%)
  waiting for transfers between devices  51.6 us (8%)
  matrix products  46 us (8%)
  loops' own time  41.1 us (7%)
  blocking collectives  21.5 us (4%)
  starting transfers between devices  9 us (1%)
    another operation x64, other arithmetic  294 us
    slice x64, local copies, waits for them, and re-layouts, frequency_term(): spectrum_pair[0][None, :] * blade_mask  65.3 us
    another operation x1, loops' own time, body(): partial_value = lax.map(per_frequency, (frequencies, spectra_pairs))  41.1 us
    dynamic_slice x64, local copies, waits for them, and re-layouts, body(): partial_value = lax.map(per_frequency, (frequencies, spectra_pairs))  38.9 us
    all_to_all x1, waiting for transfers between devices, body(): lax.all_to_all(local_spec.reshape(2 * NF, 1, item_count), 'freq', split_a...  26.3 us
    all_to_all x1, waiting for transfers between devices, body(): lax.all_to_all(shaped, 'freq', split_axis=1, concat_axis=0, tiled=True)  25.4 us
    dot_general x64, matrix products, frequency_term(): lax.dot_general(weighted, green_matrix, (((1,), (1,)), ((), ())), preferr...  23.8 us
    dot_general x1, matrix products, body(): jnp.dot(dft_table, flat, preferred_element_type=jnp.float32)  22.1 us
  transfers between devices with their start and end apart: 2, of which 2 were waited for; matrix products, arithmetic and copies ran while one was open for 0% of the time, Pallas kernels for 0%

profile of v1, /device:TPU:0, one launch (start us, length us, event | category | flops | bytes accessed | tf_op | source)
XLA Modules:
  0.0 605.7 jit_solution(17875584492578940822)
XLA Ops:
  4.1 5.2 all-to-all-start
  10.6 25.4 %all-to-all-done = bf16[128,8,1024]{0,2,1:T(8,128)(2,1)S(1)} async-done(((bf16[128,8,1024]{0,2,1:T(8,128)(2,1)}), bf16[128,8,1024]{0,2,1:T(8,128)(2,1)S(1)}, u32[]{:S(2)}, u32[]{:S(2)}) %all-to-all-start) | async-done | bytes 2097184 | tf_op jit(solution)/shard_map/all_to_all | solution.py:61
  38.5 22.1 %convert_bitcast_fusion = bf16[1024,1,1024]{2,0,1:T(8,128)(2,1)} fusion(bf16[1024,1024]{1,0:T(8,128)(2,1)} %bitcast.39, s32[1024]{0:T(1024)S(1)} %add_select_fusion.1, pred[1024]{0:T(1024)(128)(4,1)S(1)} %fusion.32), kind=kOutput, calls=%fused_computation.37 | convolution fusion | flops 2167406592 | bytes 4199424 | tf_op jit(solution)/shard_map/dot_general | solution.py:64
  72.8 26.3 %all-to-all-done.1 = bf16[8,2,65536]{2,1,0:T(2,128)(2,1)S(1)} async-done(((bf16[8,2,65536]{2,1,0:T(2,128)(2,1)}), bf16[8,2,65536]{2,1,0:T(2,128)(2,1)S(1)}, u32[]{:S(2)}, u32[]{:S(2)}) %all-to-all-start.1) | async-done | bytes 2097184 | tf_op jit(solution)/shard_map/all_to_all | solution.py:65
  110.4 472.7 %while.12 = (s32[]{:T(128)}, f32[64,4,2,32]{3,1,2,0:T(4,128)S(1)}, bf16[64,2,8192]{2,1,0:T(2,128)(2,1)}, s32[64]{0:T(128)S(1)}, s32[8192]{0:T(1024)S(1)}, /*inde...) while((s32[]{:T(128)}, f32[64,4,2,32]{3,1,2,0:T(4,128)S(1)}, ...), condition=%wide.region_1.2_spmd.clone.clone, body=%wide.region_0.1_spmd.clone.clone.sunk | while | flops 15041029 | bytes 2602569 | solution.py:78
  126.4 4.6 multiply_convert_fusion.7
  133.8 4.6 multiply_convert_fusion.7
  163.4 4.6 multiply_convert_fusion.7
  170.7 4.6 multiply_convert_fusion.7
  192.9 4.6 multiply_convert_fusion.7
  200.3 4.6 multiply_convert_fusion.7
  229.8 4.6 multiply_convert_fusion.7
  237.2 4.6 multiply_convert_fusion.7
  266.8 4.6 multiply_convert_fusion.7
  274.2 4.6 multiply_convert_fusion.7
  303.7 4.6 multiply_convert_fusion.7
  311.1 4.6 multiply_convert_fusion.7
  333.2 4.6 multiply_convert_fusion.7
  340.6 4.6 multiply_convert_fusion.7
  370.2 4.6 multiply_convert_fusion.7
  377.6 4.6 multiply_convert_fusion.7
  407.1 4.6 multiply_convert_fusion.7
  414.5 4.6 multiply_convert_fusion.7
  444.0 4.6 multiply_convert_fusion.7
  451.4 4.6 multiply_convert_fusion.7
  473.6 4.6 multiply_convert_fusion.7
  481.0 4.6 multiply_convert_fusion.7
  510.5 4.6 multiply_convert_fusion.7
  517.9 4.6 multiply_convert_fusion.7
  547.5 4.6 multiply_convert_fusion.7
  554.8 4.6 multiply_convert_fusion.7
  583.2 21.5 %all-gather = f32[256,4,2,32]{3,1,2,0:T(4,128)S(1)} all-gather(f32[64,4,2,32]{3,1,2,0:T(4,128)S(1)} %get-tuple-element.42), channel_id=2, replica_groups=mesh['grp'=4,'freq'=8] {'grp'}, dimensions={0}, use_global_device_ids=true | all-gather | bytes 327680 | tf_op jit(solution)/shard_map/all_gather | solution.py:79
  (453 shorter events, 344.8 us)
Async XLA Ops:
  0.0 9.3 %copy-start.2 = (f32[3,2048]{1,0:T(4,128)S(1)}, f32[3,2048]{1,0:T(4,128)}, u32[]{:S(2)}) copy-start(f32[3,2048]{1,0:T(4,128)} %param.10) | copy-start | bytes 73732
  0.0 9.7 %copy-start.3 = (s32[32]{0:T(128)S(1)}, s32[32]{0:T(128)}, u32[]{:S(2)}) copy-start(s32[32]{0:T(128)} %param.11) | copy-start | bytes 388
  4.1 31.8 %all-to-all-start = ((bf16[128,8,1024]{0,2,1:T(8,128)(2,1)}), bf16[128,8,1024]{0,2,1:T(8,128)(2,1)S(1)}, u32[]{:S(2)}, u32[]{:S(2)}) async-start(bf16[128,8,1024]{0,2,1:T(8,128)(2,1)} %bitcast.37), calls=%async_computation | async-start | bytes 4194304 | tf_op jit(solution)/shard_map/all_to_all | solution.py:61
  65.1 7.6 %copy-start.1 = (f32[3,8192]{1,0:T(4,128)S(1)}, f32[3,8192]{1,0:T(4,128)}, u32[]{:S(2)}) copy-start(f32[3,8192]{1,0:T(4,128)} %param.8) | copy-start | bytes 294916
  68.9 30.2 %all-to-all-start.1 = ((bf16[8,2,65536]{2,1,0:T(2,128)(2,1)}), bf16[8,2,65536]{2,1,0:T(2,128)(2,1)S(1)}, u32[]{:S(2)}, u32[]{:S(2)}) async-start(bf16[8,2,65536]{2,1,0:T(2,128)(2,1)} %reshape.64), calls=%async_computation.1 | async-start | bytes 4194304 | tf_op jit(solution)/shard_map/all_to_all | solution.py:65
  106.5 4.0 copy-start
